TPU v7x, 512 devices: a whole 4x8x8 slice. The times are simulated.
512 devices in a mesh: gx: 64 (over z_hi, y, core), gy: 8 (over z_lo, x).
Axes of the slice: x: 4, y: 8, z: 8 (z_hi: 4, z_lo: 2; z = z_hi * 2 + z_lo), core: 2. Of those that a mesh axis runs over, the one named last changes fastest.
Arguments:
- field: bfloat16 [1, 512, 512, 128], P(None, 'gx', 'gy'), may hold values from -6 to 6
- conv_weight: bfloat16 [3, 3, 128, 128], replicated, may hold values from -0.1875 to 0.1875
- qkv_weight: bfloat16 [128, 384], replicated, may hold values from -4 to 4
- out_weight: bfloat16 [128, 128], replicated, may hold values from -0.5 to 0.5
Outputs:
- result: bfloat16 [1, 512, 512, 128], P(None, 'gx', 'gy')
All inputs are finite; a program needn't handle non-finite values.
Results may differ from a plain program's by a relative error of at most 0.0064.
Values may be sent and summed in bfloat16 or wider, within the bound.
No kernel may reach another device: no remote copies, remote signals or barrier semaphores. Data moves between devices by JAX's collectives and lax.ppermute only.
A program may use at most 64 MiB of HBM per device.

v0:
```python
import jax
import jax.numpy as jnp
from jax import lax
from jax.sharding import PartitionSpec as P

HEADS = 4
HEAD = 32


def padded_2(cells, sides, width):
    for axis, dim in sides:
        count = lax.axis_size(axis)
        head = lax.slice_in_dim(cells, 0, width, axis=dim)
        tail = lax.slice_in_dim(cells, cells.shape[dim] - width, cells.shape[dim], axis=dim)
        cells = jnp.concatenate(
            [
                lax.ppermute(tail, axis, [(i, (i + 1) % count) for i in range(count)]),
                cells,
                lax.ppermute(head, axis, [((i + 1) % count, i) for i in range(count)]),
            ],
            axis=dim,
        )
    return cells


def head_attend(parts):
    query, keyed, valued = parts
    scores = jnp.einsum("zqyd,zkyd->zyqk", query, keyed, preferred_element_type=jnp.float32)
    scores = scores / jnp.sqrt(jnp.float32(HEAD))
    top = jnp.max(scores, axis=-1, keepdims=True)
    expo = jnp.exp(scores - top)
    probs = (expo / jnp.sum(expo, axis=-1, keepdims=True)).astype(jnp.bfloat16)
    mixed = jnp.einsum("zyqk,zkyd->zqyd", probs, valued, preferred_element_type=jnp.float32)
    return mixed.astype(jnp.bfloat16)


def split_heads(block):
    planes, length, cols, width = block.shape
    return jnp.moveaxis(block.reshape(planes, length, cols, HEADS, width // HEADS), 3, 0)


def attend_lines(normed, qkv_weight):
    planes, length, cols, width = normed.shape
    qkv = jnp.dot(normed.reshape(-1, width), qkv_weight, preferred_element_type=jnp.float32)
    qkv = qkv.astype(jnp.bfloat16).reshape(planes, length, cols, 3 * width)
    query = split_heads(qkv[..., :width])
    keyed = split_heads(qkv[..., width : 2 * width])
    valued = split_heads(qkv[..., 2 * width :])
    mixed = lax.map(head_attend, (query, keyed, valued))
    return jnp.moveaxis(mixed, 0, 3).reshape(planes, length, cols, width)


def return_cells(block):
    return lax.all_to_all(block, "gx", split_axis=1, concat_axis=2, tiled=True)


def convolve(padded, conv_weight, rows, cols):
    planes = padded.shape[0]
    width = padded.shape[3]
    stem = jnp.zeros((planes, rows, cols, width), jnp.float32)
    for a in range(3):
        for b in range(3):
            window = padded[:, a : a + rows, b : b + cols, :]
            part = jnp.dot(
                window.reshape(-1, width), conv_weight[a, b], preferred_element_type=jnp.float32
            )
            stem = stem + part.reshape(planes, rows, cols, width)
    return stem


def normalize(stem):
    mean = jnp.mean(stem, axis=-1, keepdims=True)
    varia = jnp.mean((stem - mean) ** 2, axis=-1, keepdims=True)
    return ((stem - mean) / jnp.sqrt(varia + 1e-05)).astype(jnp.bfloat16)


def finish(stem, attended, out_weight):
    width = stem.shape[3]
    projected = jnp.dot(attended.reshape(-1, width), out_weight, preferred_element_type=jnp.float32)
    return (stem + projected.reshape(stem.shape)).astype(jnp.bfloat16)


def on_device(field, conv_weight, qkv_weight, out_weight):
    planes, rows, cols, width = field.shape
    padded = padded_2(field, (("gx", 1), ("gy", 2)), 1)
    stem = convolve(padded, conv_weight, rows, cols)
    normed = normalize(stem)
    attended = return_cells(
        attend_lines(
            lax.all_to_all(normed, "gx", split_axis=2, concat_axis=1, tiled=True), qkv_weight
        )
    )
    return finish(stem, attended, out_weight)


def solution(mesh):
    placed = (P(None, "gx", "gy", None), P(), P(), P())
    return jax.shard_map(
        on_device, mesh=mesh, in_specs=placed, out_specs=P(None, "gx", "gy", None), check_vma=False
    )
```

profile of v0, /device:TPU:7, one launch (start us, length us, event | category | flops | bytes accessed | tf_op | source)
XLA Modules:
  0.0 76.4 jit_solution(8873037923194557447)
XLA Ops:
  0.0 0.8 %fusion.78 = (bf16[1,1,64,128]{3,2,1,0:T(8,128)(2,1)S(1)}, bf16[1,1,64,128]{3,2,1,0:T(8,128)(2,1)S(1)}) fusion(bf16[1,8,64,128]{3,2,1,0:T(8,128)(2,1)} %param.6), kind=kLoop, calls=%fused_computation.102 | loop fusion | bytes 65536 | tf_op jit(solution)/shard_map/slice | solution.py:13
  0.8 3.8 %collective-permute-start = (bf16[1,1,64,128]{3,2,1,0:T(8,128)(2,1)S(1)}, bf16[1,1,64,128]{3,2,1,0:T(8,128)(2,1)S(1)}, u32[]{:S(2)}, u32[]{:S(2)}) collective-permute-start(bf16[1,1,64,128]{3,2,1,0:T(8,128)(2,1)S(1)} %get-tuple-element.51), channel_id=1, source_target_pairs={{0,8},{8,16},{16,24},{24,32},{32,40},{40,48},{48,56},{56,64},{64,7... | collective-permute-start | bytes 49160 | tf_op jit(solution)/shard_map/ppermute | solution.py:17
  4.5 1.9 %collective-permute-start.1 = (bf16[1,1,64,128]{3,2,1,0:T(8,128)(2,1)S(1)}, bf16[1,1,64,128]{3,2,1,0:T(8,128)(2,1)S(1)}, u32[]{:S(2)}, u32[]{:S(2)}) collective-permute-start(bf16[1,1,64,128]{3,2,1,0:T(8,128)(2,1)S(1)} %get-tuple-element.50), channel_id=1, source_target_pairs={{8,0},{16,8},{24,16},{32,24},{40,32},{48,40},{56,48},{64,56},{72,6... | collective-permute-start | bytes 49160 | tf_op jit(solution)/shard_map/ppermute | solution.py:19
  6.5 0.0 collective-permute-done
  6.5 0.0 copy-start.1
  6.5 1.0 %constant_dynamic-update-slice_fusion.1 = bf16[1,10,64,128]{3,2,1,0:T(8,128)(2,1)S(1)} fusion(bf16[1,10,64,128]{3,2,1,0:T(8,128)(2,1)S(1)} %constant_dynamic-update-slice_fusion.2, bf16[1,8,64,128]{3,2,1,0:T(8,128)(2,1)} %param.6), kind=kLoop, calls=%fused_computation.87 | loop fusion | bytes 262144
  7.5 0.0 copy-start.2
  7.5 2.1 %collective-permute-done.1 = bf16[1,1,64,128]{3,2,1,0:T(8,128)(2,1)S(1)} collective-permute-done((bf16[1,1,64,128]{3,2,1,0:T(8,128)(2,1)S(1)}, bf16[1,1,64,128]{3,2,1,0:T(8,128)(2,1)S(1)}, u32[]{:S(2)}, u32[]{:S(2)}) %collective-permute-start.1) | collective-permute-done | bytes 16416 | tf_op jit(solution)/shard_map/ppermute | solution.py:19
  9.6 3.9 %collective-permute-start.2 = (bf16[1,10,1,128]{3,2,1,0:T(2,128)(2,1)S(1)}, bf16[1,10,1,128]{3,2,1,0:T(2,128)(2,1)S(1)}, u32[]{:S(2)}, u32[]{:S(2)}) collective-permute-start(bf16[1,10,1,128]{3,2,1,0:T(2,128)(2,1)S(1)} %get-tuple-element.48), channel_id=1, source_target_pairs={{0,1},{1,2},{2,3},{3,4},{4,5},{5,6},{6,7},{7,0},{8,9},{9,10},{10,1... | collective-permute-start | bytes 7688 | tf_op jit(solution)/shard_map/ppermute | solution.py:17
  13.5 1.9 %collective-permute-start.3 = (bf16[1,10,1,128]{3,2,1,0:T(2,128)(2,1)S(1)}, bf16[1,10,1,128]{3,2,1,0:T(2,128)(2,1)S(1)}, u32[]{:S(2)}, u32[]{:S(2)}) collective-permute-start(bf16[1,10,1,128]{3,2,1,0:T(2,128)(2,1)S(1)} %get-tuple-element.49), channel_id=1, source_target_pairs={{1,0},{2,1},{3,2},{4,3},{5,4},{6,5},{7,6},{0,7},{9,8},{10,9},{11,1... | collective-permute-start | bytes 7688 | tf_op jit(solution)/shard_map/ppermute | solution.py:19
  15.5 0.9 %fusion.40 = f32[8,64,128]{2,1,0:T(8,128)S(1)} fusion(bf16[1,8,64,128]{3,2,1,0:T(8,128)(2,1)S(1)} %copy-done.1, bf16[1,1,64,128]{3,2,1,0:T(8,128)(2,1)S(1)} %collective-permute-done, bf16[3,3,128,128]{3,2,1,0:T(8,128)(2,1)} %param.7), kind=kOutput, calls=%fused_computation.59 | convolution fusion | flops 16842752 | bytes 442368 | tf_op jit(solution)/shard_map/dot_general | solution.py:64
  16.4 0.2 fusion.33
  16.6 0.2 convolution_add_fusion.6
  16.8 3.2 %collective-permute-done.3 = bf16[1,10,1,128]{3,2,1,0:T(2,128)(2,1)S(1)} collective-permute-done((bf16[1,10,1,128]{3,2,1,0:T(2,128)(2,1)S(1)}, bf16[1,10,1,128]{3,2,1,0:T(2,128)(2,1)S(1)}, u32[]{:S(2)}, u32[]{:S(2)}) %collective-permute-start.3) | collective-permute-done | bytes 2592 | tf_op jit(solution)/shard_map/ppermute | solution.py:19
  20.0 0.2 convolution_add_fusion.5
  20.2 0.2 convolution_add_fusion.4
  20.4 0.2 convolution_add_fusion.3
  20.6 0.2 fusion.29
  20.7 0.2 convolution_add_fusion.2
  20.9 0.3 fusion.79
  21.2 0.3 multiply_reduce_fusion
  21.5 0.2 fusion.47
  21.7 0.7 copy.21
  22.5 16.7 %all-to-all-start = ((bf16[1,8,64,128]{3,1,0,2:T(8,128)(2,1)}), bf16[1,8,64,128]{3,1,0,2:T(8,128)(2,1)S(1)}, u32[]{:S(2)}, u32[]{:S(2)}) async-start(bf16[1,8,64,128]{3,1,0,2:T(8,128)(2,1)} %copy.21), calls=%async_computation | async-start | bytes 262144 | tf_op jit(solution)/shard_map/all_to_all | solution.py:90
  39.2 12.8 %all-to-all-done = bf16[1,8,64,128]{3,1,0,2:T(8,128)(2,1)S(1)} async-done(((bf16[1,8,64,128]{3,1,0,2:T(8,128)(2,1)}), bf16[1,8,64,128]{3,1,0,2:T(8,128)(2,1)S(1)}, u32[]{:S(2)}, u32[]{:S(2)}) %all-to-all-start) | async-done | bytes 131104 | tf_op jit(solution)/shard_map/all_to_all | solution.py:90
  51.9 0.3 fusion.11
  52.3 3.4 %while.10 = (s32[]{:T(128)}, bf16[4,1,512,1,32]{2,4,3,1,0:T(8,128)(2,1)S(1)}, bf16[4,1,512,1,32]{2,4,3,1,0:T(8,128)(2,1)S(1)}, bf16[4,1,512,1,32]{2,4,3,1,0:T(8,...) while((s32[]{:T(128)}, bf16[4,1,512,1,32]{2,4,3,1,0:T(8,128)(2,1)S(1)}, ...), condition=%wide.region_5.6_spmd, body=%wide.region_2.5_spmd.sunk | while | flops 35404800 | bytes 3289157 | solution.py:49
  52.3 0.4 fusion.86
  52.7 0.2 fusion.87
  52.8 0.3 fusion.88
  53.1 0.4 fusion.86
  53.5 0.2 fusion.87
  53.7 0.3 fusion.88
  54.0 0.4 fusion.86
  54.4 0.2 fusion.87
  54.6 0.3 fusion.88
  54.9 0.4 fusion.86
  55.2 0.2 fusion.87
  55.4 0.3 fusion.88
  55.7 0.2 copy.26
  55.9 0.5 broadcast.39
  56.4 1.4 %reduce.8 = bf16[512,128]{1,0:T(8,128)(2,1)S(1)} reduce(bf16[512,1,1,128]{3,2,1,0:T(2,128)(2,1)S(1)} %bitcast.152, bf16[]{:T(256)} %broadcast.39), dimensions={1,2}, to_apply=%bitcast.132.reduce_sub_computation | reduce | bytes 262146
  57.8 0.1 reshape.154
  57.9 16.8 %all_to_all.30 = bf16[64,2,512]{2,1,0:T(2,128)(2,1)S(1)} all-to-all(bf16[64,2,512]{2,1,0:T(2,128)(2,1)S(1)} %reshape.154), channel_id=1, replica_groups=mesh['gx'=64,'gy'=8] {'gx'}, dimensions={0} | all-to-all | bytes 262144 | tf_op jit(solution)/shard_map/all_to_all | solution.py:54
  74.7 0.1 reshape.155
  74.8 0.0 copy-start.3
  74.9 0.7 copy-done.3
  75.6 0.8 %fusion.15 = bf16[1,8,64,128]{3,2,1,0:T(8,128)(2,1)} fusion(f32[8,64,128]{2,1,0:T(8,128)S(1)} %get-tuple-element.53, bf16[1,64,8,1,128]{4,2,1,3,0:T(8,128)(2,1)S(1)} %bitcast.156, bf16[128,128]{1,0:T(8,128)(2,1)S(1)} %copy-done.3), kind=kOutput, calls=%fused_computation.27 | convolution fusion | flops 16908288 | bytes 557056 | tf_op jit(solution)/shard_map/dot_general | solution.py:79
  (13 shorter events, 0.1 us)
Async XLA Ops:
  0.0 51.9 %copy-start = (bf16[128,384]{1,0:T(8,128)(2,1)S(1)}, bf16[128,384]{1,0:T(8,128)(2,1)}, u32[]{:S(2)}) copy-start(bf16[128,384]{1,0:T(8,128)(2,1)} %param.8) | copy-start | bytes 294916
  0.8 5.7 %collective-permute-start = (bf16[1,1,64,128]{3,2,1,0:T(8,128)(2,1)S(1)}, bf16[1,1,64,128]{3,2,1,0:T(8,128)(2,1)S(1)}, u32[]{:S(2)}, u32[]{:S(2)}) collective-permute-start(bf16[1,1,64,128]{3,2,1,0:T(8,128)(2,1)S(1)} %get-tuple-element.51), channel_id=1, source_target_pairs={{0,8},{8,16},{16,24},{24,32},{32,40},{40,48},{48,56},{56,64},{64,7... | collective-permute-start | bytes 49160 | tf_op jit(solution)/shard_map/ppermute | solution.py:17
  4.5 5.1 %collective-permute-start.1 = (bf16[1,1,64,128]{3,2,1,0:T(8,128)(2,1)S(1)}, bf16[1,1,64,128]{3,2,1,0:T(8,128)(2,1)S(1)}, u32[]{:S(2)}, u32[]{:S(2)}) collective-permute-start(bf16[1,1,64,128]{3,2,1,0:T(8,128)(2,1)S(1)} %get-tuple-element.50), channel_id=1, source_target_pairs={{8,0},{16,8},{24,16},{32,24},{40,32},{48,40},{56,48},{64,56},{72,6... | collective-permute-start | bytes 49160 | tf_op jit(solution)/shard_map/ppermute | solution.py:19
  6.5 9.0 %copy-start.1 = (bf16[1,8,64,128]{3,2,1,0:T(8,128)(2,1)S(1)}, bf16[1,8,64,128]{3,2,1,0:T(8,128)(2,1)}, u32[]{:S(2)}) copy-start(bf16[1,8,64,128]{3,2,1,0:T(8,128)(2,1)} %param.6) | copy-start | bytes 393220
  7.5 8.9 %copy-start.2 = (bf16[3,3,128,128]{3,2,1,0:T(8,128)(2,1)S(1)}, bf16[3,3,128,128]{3,2,1,0:T(8,128)(2,1)}, u32[]{:S(2)}) copy-start(bf16[3,3,128,128]{3,2,1,0:T(8,128)(2,1)} %param.7) | copy-start | bytes 884740
  9.6 7.0 %collective-permute-start.2 = (bf16[1,10,1,128]{3,2,1,0:T(2,128)(2,1)S(1)}, bf16[1,10,1,128]{3,2,1,0:T(2,128)(2,1)S(1)}, u32[]{:S(2)}, u32[]{:S(2)}) collective-permute-start(bf16[1,10,1,128]{3,2,1,0:T(2,128)(2,1)S(1)} %get-tuple-element.48), channel_id=1, source_target_pairs={{0,1},{1,2},{2,3},{3,4},{4,5},{5,6},{6,7},{7,0},{8,9},{9,10},{10,1... | collective-permute-start | bytes 7688 | tf_op jit(solution)/shard_map/ppermute | solution.py:17
  13.5 6.5 %collective-permute-start.3 = (bf16[1,10,1,128]{3,2,1,0:T(2,128)(2,1)S(1)}, bf16[1,10,1,128]{3,2,1,0:T(2,128)(2,1)S(1)}, u32[]{:S(2)}, u32[]{:S(2)}) collective-permute-start(bf16[1,10,1,128]{3,2,1,0:T(2,128)(2,1)S(1)} %get-tuple-element.49), channel_id=1, source_target_pairs={{1,0},{2,1},{3,2},{4,3},{5,4},{6,5},{7,6},{0,7},{9,8},{10,9},{11,1... | collective-permute-start | bytes 7688 | tf_op jit(solution)/shard_map/ppermute | solution.py:19
  22.5 29.5 %all-to-all-start = ((bf16[1,8,64,128]{3,1,0,2:T(8,128)(2,1)}), bf16[1,8,64,128]{3,1,0,2:T(8,128)(2,1)S(1)}, u32[]{:S(2)}, u32[]{:S(2)}) async-start(bf16[1,8,64,128]{3,1,0,2:T(8,128)(2,1)} %copy.21), calls=%async_computation | async-start | bytes 262144 | tf_op jit(solution)/shard_map/all_to_all | solution.py:90
  74.8 0.8 copy-start.3
where the time goes:
time: 76.9 us; the launch traced here: 76.4 us
  starting transfers between devices  28.2 us (37%)
  waiting for transfers between devices  18.1 us (24%)
  blocking collectives  16.8 us (22%)
  matrix products  6.15 us (8%)
  local copies, waits for them, and re-layouts  4.16 us (5%)
  other arithmetic  2.67 us (3%)
    all_to_all x1, blocking collectives, return_cells(): return lax.all_to_all(block, 'gx', split_axis=1, concat_axis=2, tiled=True)  16.8 us
    all_to_all x1, starting transfers between devices, on_device(): lax.all_to_all(normed, 'gx', split_axis=2, concat_axis=1, tiled=True)  16.7 us
    all_to_all x1, waiting for transfers between devices, on_device(): lax.all_to_all(normed, 'gx', split_axis=2, concat_axis=1, tiled=True)  12.8 us
    ppermute x2, starting transfers between devices, padded_2(): lax.ppermute(tail, axis, [(i, (i + 1) % count) for i in range(count)])  7.67 us
    ppermute x2, waiting for transfers between devices, padded_2(): lax.ppermute(head, axis, [((i + 1) % count, i) for i in range(count)])  5.32 us
    ppermute x2, starting transfers between devices, padded_2(): lax.ppermute(head, axis, [((i + 1) % count, i) for i in range(count)])  3.84 us
    unnamed x14, local copies, waits for them, and re-layouts  2.42 us
    dot_general x9, matrix products, convolve(): jnp.dot(window.reshape(-1, width), conv_weight[a, b], preferred_element_t...  2.4 us
  transfers between devices with their start and end apart: 5, of which 3 were waited for; matrix products, arithmetic and copies ran while one was open for 3% of the time, Pallas kernels for 0%

commit v1 on v0

--- a/solution.py
+++ b/solution.py
@@ -5,6 +5,15 @@
 
 HEADS = 4
 HEAD = 32
+apply_unit = lambda patch, dev_axis: jnp.concatenate(
+    jax.lax.all_to_all(
+        jnp.stack(jnp.split(patch, jax.lax.axis_size(dev_axis), axis=2)),
+        dev_axis,
+        split_axis=0,
+        concat_axis=0,
+    ),
+    1,
+)
 
 
 def padded_2(cells, sides, width):
@@ -85,11 +94,7 @@
     padded = padded_2(field, (("gx", 1), ("gy", 2)), 1)
     stem = convolve(padded, conv_weight, rows, cols)
     normed = normalize(stem)
-    attended = return_cells(
-        attend_lines(
-            lax.all_to_all(normed, "gx", split_axis=2, concat_axis=1, tiled=True), qkv_weight
-        )
-    )
+    attended = return_cells(attend_lines(apply_unit(normed, "gx"), qkv_weight))
     return finish(stem, attended, out_weight)
 
 

time: 76.9 us -> 114 us (1.48)
  local copies, waits for them, and re-layouts: 4.16 us -> 40.7 us
    unnamed x14 -> x77, local copies, waits for them, and re-layouts: 2.42 us -> 38.9 us
  transfers between devices with their start and end apart: 5 -> 5, of which waited for: 3 -> 3; matrix products, arithmetic and copies ran while one was open for 3% -> 2% of each run, Pallas kernels for 0% -> 0%
where the time goes in v1:
time: 114 us; the launch traced here: 113 us
  local copies, waits for them, and re-layouts  40.7 us (36%)
  starting transfers between devices  28.2 us (25%)
  waiting for transfers between devices  18.1 us (16%)
  blocking collectives  16.9 us (15%)
  matrix products  6.14 us (5%)
  other arithmetic  2.67 us (2%)
    unnamed x77, local copies, waits for them, and re-layouts  38.9 us
    all_to_all x1, blocking collectives, return_cells(): return lax.all_to_all(block, 'gx', split_axis=1, concat_axis=2, tiled=True)  16.9 us
    all_to_all x1, starting transfers between devices, jax.lax.all_to_all(jnp.stack(jnp.split(patch, jax.lax.axis_size(dev_axis)...  16.7 us
    all_to_all x1, waiting for transfers between devices, jax.lax.all_to_all(jnp.stack(jnp.split(patch, jax.lax.axis_size(dev_axis)...  12.8 us
    ppermute x2, starting transfers between devices, padded_2(): lax.ppermute(tail, axis, [(i, (i + 1) % count) for i in range(count)])  7.67 us
    ppermute x2, waiting for transfers between devices, padded_2(): lax.ppermute(head, axis, [((i + 1) % count, i) for i in range(count)])  5.32 us
    ppermute x2, starting transfers between devices, padded_2(): lax.ppermute(head, axis, [((i + 1) % count, i) for i in range(count)])  3.84 us
    dot_general x9, matrix products, convolve(): jnp.dot(window.reshape(-1, width), conv_weight[a, b], preferred_element_t...  2.4 us
  transfers between devices with their start and end apart: 5, of which 3 were waited for; matrix products, arithmetic and copies ran while one was open for 2% of the time, Pallas kernels for 0%

profile of v1, /device:TPU:7, one launch (start us, length us, event | category | flops | bytes accessed | tf_op | source)
XLA Modules:
  0.0 113.1 jit_solution(4138467299828289453)
XLA Ops:
  0.0 0.8 fusion.82
  0.8 3.8 %collective-permute-start = (bf16[1,1,64,128]{3,2,1,0:T(8,128)(2,1)S(1)}, bf16[1,1,64,128]{3,2,1,0:T(8,128)(2,1)S(1)}, u32[]{:S(2)}, u32[]{:S(2)}) collective-permute-start(bf16[1,1,64,128]{3,2,1,0:T(8,128)(2,1)S(1)} %get-tuple-element.125), channel_id=1, source_target_pairs={{0,8},{8,16},{16,24},{24,32},{32,40},{40,48},{48,56},{56,64},{64,7... | collective-permute-start | bytes 49160 | tf_op jit(solution)/shard_map/ppermute | solution.py:26
  4.5 1.9 %collective-permute-start.1 = (bf16[1,1,64,128]{3,2,1,0:T(8,128)(2,1)S(1)}, bf16[1,1,64,128]{3,2,1,0:T(8,128)(2,1)S(1)}, u32[]{:S(2)}, u32[]{:S(2)}) collective-permute-start(bf16[1,1,64,128]{3,2,1,0:T(8,128)(2,1)S(1)} %get-tuple-element.124), channel_id=1, source_target_pairs={{8,0},{16,8},{24,16},{32,24},{40,32},{48,40},{56,48},{64,56},{72,6... | collective-permute-start | bytes 49160 | tf_op jit(solution)/shard_map/ppermute | solution.py:28
  6.5 1.0 constant_dynamic-update-slice_fusion.1
  7.5 2.1 %collective-permute-done.1 = bf16[1,1,64,128]{3,2,1,0:T(8,128)(2,1)S(1)} collective-permute-done((bf16[1,1,64,128]{3,2,1,0:T(8,128)(2,1)S(1)}, bf16[1,1,64,128]{3,2,1,0:T(8,128)(2,1)S(1)}, u32[]{:S(2)}, u32[]{:S(2)}) %collective-permute-start.1) | collective-permute-done | bytes 16416 | tf_op jit(solution)/shard_map/ppermute | solution.py:28
  9.6 3.9 %collective-permute-start.2 = (bf16[1,10,1,128]{3,2,1,0:T(2,128)(2,1)S(1)}, bf16[1,10,1,128]{3,2,1,0:T(2,128)(2,1)S(1)}, u32[]{:S(2)}, u32[]{:S(2)}) collective-permute-start(bf16[1,10,1,128]{3,2,1,0:T(2,128)(2,1)S(1)} %get-tuple-element.58), channel_id=1, source_target_pairs={{0,1},{1,2},{2,3},{3,4},{4,5},{5,6},{6,7},{7,0},{8,9},{9,10},{10,1... | collective-permute-start | bytes 7688 | tf_op jit(solution)/shard_map/ppermute | solution.py:26
  13.5 1.9 %collective-permute-start.3 = (bf16[1,10,1,128]{3,2,1,0:T(2,128)(2,1)S(1)}, bf16[1,10,1,128]{3,2,1,0:T(2,128)(2,1)S(1)}, u32[]{:S(2)}, u32[]{:S(2)}) collective-permute-start(bf16[1,10,1,128]{3,2,1,0:T(2,128)(2,1)S(1)} %get-tuple-element.59), channel_id=1, source_target_pairs={{1,0},{2,1},{3,2},{4,3},{5,4},{6,5},{7,6},{0,7},{9,8},{10,9},{11,1... | collective-permute-start | bytes 7688 | tf_op jit(solution)/shard_map/ppermute | solution.py:28
  15.5 0.9 fusion.40
  16.8 3.2 %collective-permute-done.3 = bf16[1,10,1,128]{3,2,1,0:T(2,128)(2,1)S(1)} collective-permute-done((bf16[1,10,1,128]{3,2,1,0:T(2,128)(2,1)S(1)}, bf16[1,10,1,128]{3,2,1,0:T(2,128)(2,1)S(1)}, u32[]{:S(2)}, u32[]{:S(2)}) %collective-permute-start.3) | collective-permute-done | bytes 2592 | tf_op jit(solution)/shard_map/ppermute | solution.py:28
  22.0 0.6 constant_dynamic-update-slice_fusion.66
  22.6 0.6 constant_dynamic-update-slice_fusion.65
  23.1 0.6 constant_dynamic-update-slice_fusion.64
  23.7 0.6 constant_dynamic-update-slice_fusion.63
  24.3 0.6 constant_dynamic-update-slice_fusion.62
  24.9 0.6 constant_dynamic-update-slice_fusion.61
  25.5 0.6 constant_dynamic-update-slice_fusion.60
  26.0 0.6 constant_dynamic-update-slice_fusion.59
  26.6 0.6 constant_dynamic-update-slice_fusion.58
  27.2 0.6 constant_dynamic-update-slice_fusion.57
  27.8 0.6 constant_dynamic-update-slice_fusion.56
  28.4 0.6 constant_dynamic-update-slice_fusion.55
  28.9 0.6 constant_dynamic-update-slice_fusion.54
  29.5 0.6 constant_dynamic-update-slice_fusion.53
  30.1 0.6 constant_dynamic-update-slice_fusion.52
  30.7 0.6 constant_dynamic-update-slice_fusion.51
  31.3 0.6 constant_dynamic-update-slice_fusion.50
  31.8 0.6 constant_dynamic-update-slice_fusion.49
  32.4 0.6 constant_dynamic-update-slice_fusion.48
  33.0 0.6 constant_dynamic-update-slice_fusion.47
  33.6 0.6 constant_dynamic-update-slice_fusion.46
  34.2 0.6 constant_dynamic-update-slice_fusion.45
  34.7 0.6 constant_dynamic-update-slice_fusion.44
  35.3 0.6 constant_dynamic-update-slice_fusion.43
  35.9 0.6 constant_dynamic-update-slice_fusion.42
  36.5 0.6 constant_dynamic-update-slice_fusion.41
  37.1 0.6 constant_dynamic-update-slice_fusion.40
  37.6 0.6 constant_dynamic-update-slice_fusion.39
  38.2 0.6 constant_dynamic-update-slice_fusion.38
  38.8 0.6 constant_dynamic-update-slice_fusion.37
  39.4 0.6 constant_dynamic-update-slice_fusion.36
  40.0 0.6 constant_dynamic-update-slice_fusion.35
  59.1 16.7 %all-to-all-start = ((bf16[64,1,8,1,128]{4,2,3,1,0:T(8,128)(2,1)}), bf16[64,1,8,1,128]{4,2,3,1,0:T(8,128)(2,1)S(1)}, u32[]{:S(2)}, u32[]{:S(2)}) async-start(bf16[64,1,8,1,128]{4,2,3,1,0:T(8,128)(2,1)} %constant_dynamic-update-slice_fusion.3), calls=%async_computation | async-start | bytes 262144 | tf_op jit(solution)/shard_map/all_to_all | solution.py:9
  75.8 12.8 %all-to-all-done = bf16[64,1,8,1,128]{4,2,3,1,0:T(8,128)(2,1)S(1)} async-done(((bf16[64,1,8,1,128]{4,2,3,1,0:T(8,128)(2,1)}), bf16[64,1,8,1,128]{4,2,3,1,0:T(8,128)(2,1)S(1)}, u32[]{:S(2)}, u32[]{:S(2)}) %all-to-all-start) | async-done | bytes 131104 | tf_op jit(solution)/shard_map/all_to_all | solution.py:9
  88.9 3.4 %while.10 = (s32[]{:T(128)}, bf16[4,1,512,1,32]{2,4,3,1,0:T(8,128)(2,1)S(1)}, bf16[4,1,512,1,32]{2,4,3,1,0:T(8,128)(2,1)S(1)}, bf16[4,1,512,1,32]{2,4,3,1,0:T(8,...) while((s32[]{:T(128)}, bf16[4,1,512,1,32]{2,4,3,1,0:T(8,128)(2,1)S(1)}, ...), condition=%wide.region_5.6_spmd, body=%wide.region_2.5_spmd.sunk | while | flops 35404800 | bytes 3289157 | solution.py:58
  93.0 1.4 %reduce.8 = bf16[512,128]{1,0:T(8,128)(2,1)S(1)} reduce(bf16[512,1,1,128]{3,2,1,0:T(2,128)(2,1)S(1)} %bitcast.276, bf16[]{:T(256)} %broadcast.39), dimensions={1,2}, to_apply=%bitcast.256.reduce_sub_computation | reduce | bytes 262146
  94.5 16.9 %all_to_all.20 = bf16[64,2,512]{2,1,0:T(2,128)(2,1)S(1)} all-to-all(bf16[64,2,512]{2,1,0:T(2,128)(2,1)S(1)} %reshape.149), channel_id=1, replica_groups=mesh['gx'=64,'gy'=8] {'gx'}, dimensions={0} | all-to-all | bytes 262144 | tf_op jit(solution)/shard_map/all_to_all | solution.py:63
  111.5 0.7 copy-done.3
  112.2 0.8 fusion.15
  (80 shorter events, 25.4 us)
Async XLA Ops:
  0.0 88.6 %copy-start = (bf16[128,384]{1,0:T(8,128)(2,1)S(1)}, bf16[128,384]{1,0:T(8,128)(2,1)}, u32[]{:S(2)}) copy-start(bf16[128,384]{1,0:T(8,128)(2,1)} %param.8) | copy-start | bytes 294916
  0.8 5.7 %collective-permute-start = (bf16[1,1,64,128]{3,2,1,0:T(8,128)(2,1)S(1)}, bf16[1,1,64,128]{3,2,1,0:T(8,128)(2,1)S(1)}, u32[]{:S(2)}, u32[]{:S(2)}) collective-permute-start(bf16[1,1,64,128]{3,2,1,0:T(8,128)(2,1)S(1)} %get-tuple-element.125), channel_id=1, source_target_pairs={{0,8},{8,16},{16,24},{24,32},{32,40},{40,48},{48,56},{56,64},{64,7... | collective-permute-start | bytes 49160 | tf_op jit(solution)/shard_map/ppermute | solution.py:26
  4.5 5.1 %collective-permute-start.1 = (bf16[1,1,64,128]{3,2,1,0:T(8,128)(2,1)S(1)}, bf16[1,1,64,128]{3,2,1,0:T(8,128)(2,1)S(1)}, u32[]{:S(2)}, u32[]{:S(2)}) collective-permute-start(bf16[1,1,64,128]{3,2,1,0:T(8,128)(2,1)S(1)} %get-tuple-element.124), channel_id=1, source_target_pairs={{8,0},{16,8},{24,16},{32,24},{40,32},{48,40},{56,48},{64,56},{72,6... | collective-permute-start | bytes 49160 | tf_op jit(solution)/shard_map/ppermute | solution.py:28
  6.5 9.0 %copy-start.1 = (bf16[1,8,64,128]{3,2,1,0:T(8,128)(2,1)S(1)}, bf16[1,8,64,128]{3,2,1,0:T(8,128)(2,1)}, u32[]{:S(2)}) copy-start(bf16[1,8,64,128]{3,2,1,0:T(8,128)(2,1)} %param.6) | copy-start | bytes 393220
  7.5 8.9 %copy-start.2 = (bf16[3,3,128,128]{3,2,1,0:T(8,128)(2,1)S(1)}, bf16[3,3,128,128]{3,2,1,0:T(8,128)(2,1)}, u32[]{:S(2)}) copy-start(bf16[3,3,128,128]{3,2,1,0:T(8,128)(2,1)} %param.7) | copy-start | bytes 884740
  9.6 7.0 %collective-permute-start.2 = (bf16[1,10,1,128]{3,2,1,0:T(2,128)(2,1)S(1)}, bf16[1,10,1,128]{3,2,1,0:T(2,128)(2,1)S(1)}, u32[]{:S(2)}, u32[]{:S(2)}) collective-permute-start(bf16[1,10,1,128]{3,2,1,0:T(2,128)(2,1)S(1)} %get-tuple-element.58), channel_id=1, source_target_pairs={{0,1},{1,2},{2,3},{3,4},{4,5},{5,6},{6,7},{7,0},{8,9},{9,10},{10,1... | collective-permute-start | bytes 7688 | tf_op jit(solution)/shard_map/ppermute | solution.py:26
  13.5 6.5 %collective-permute-start.3 = (bf16[1,10,1,128]{3,2,1,0:T(2,128)(2,1)S(1)}, bf16[1,10,1,128]{3,2,1,0:T(2,128)(2,1)S(1)}, u32[]{:S(2)}, u32[]{:S(2)}) collective-permute-start(bf16[1,10,1,128]{3,2,1,0:T(2,128)(2,1)S(1)} %get-tuple-element.59), channel_id=1, source_target_pairs={{1,0},{2,1},{3,2},{4,3},{5,4},{6,5},{7,6},{0,7},{9,8},{10,9},{11,1... | collective-permute-start | bytes 7688 | tf_op jit(solution)/shard_map/ppermute | solution.py:28
  59.1 29.5 %all-to-all-start = ((bf16[64,1,8,1,128]{4,2,3,1,0:T(8,128)(2,1)}), bf16[64,1,8,1,128]{4,2,3,1,0:T(8,128)(2,1)S(1)}, u32[]{:S(2)}, u32[]{:S(2)}) async-start(bf16[64,1,8,1,128]{4,2,3,1,0:T(8,128)(2,1)} %constant_dynamic-update-slice_fusion.3), calls=%async_computation | async-start | bytes 262144 | tf_op jit(solution)/shard_map/all_to_all | solution.py:9
  111.5 0.8 copy-start.3
